TPU v7x, 32 devices: a whole 2x2x4 slice. The times are simulated.
32 devices in a mesh: dp: 8 (over z, x), mp: 4 (over y, core).
Axes of the slice: x: 2, y: 2, z: 4, core: 2. Of those that a mesh axis runs over, the one named last changes fastest.
Arguments:
- gradients: bfloat16 [8, 3584, 14336], P(None, 'dp', 'mp'), may hold values from -60 to 60
- column_slot: int32 [8, 16], replicated, may hold values from 0 to 31, as said below
- left_roots: bfloat16 [32, 4, 4, 896, 896], P('dp', 'mp'), may hold values from -1 to 5
- right_roots: bfloat16 [32, 4, 4, 896, 896], P('dp', 'mp'), may hold values from -1 to 5
Outputs:
- update: bfloat16 [8, 3584, 14336], P(None, 'dp', 'mp')
- clip_scale: float32 [], replicated
Inputs may be any that keep to these rules, and one draw needn't show every extreme that they name: `column_slot`: block column c belongs to group c // 4; over all matrices, the entries of one group's block columns are a permutation of 0 to 31.
All inputs are finite; a program needn't handle non-finite values.
Results may differ from a plain program's by a relative error of at most 0.0049.
Values may be sent and summed in bfloat16 or wider, within the bound.
A program may use at most 256 MiB of HBM per device.

v0:
```python
import jax
import jax.numpy as jnp
from jax import lax
from jax.sharding import PartitionSpec as P

D = 3584
FF = 14336
BLOCK = 896
MATRICES = 8
rms_limit = 0.25
epsilon = 1e-06


def body(gradients, column_slot, left_roots, right_roots):
    row_count = gradients.shape[1]
    local_cols = gradients.shape[2] // BLOCK
    slot_count = MATRICES * local_cols
    mp_index = lax.axis_index("mp")
    my_slots = lax.dynamic_slice_in_dim(column_slot, mp_index * local_cols, local_cols, 1).reshape(
        slot_count
    )
    columns = (
        gradients.reshape(MATRICES, row_count, local_cols, BLOCK)
        .transpose(0, 2, 1, 3)
        .reshape(slot_count, row_count, BLOCK)
    )
    send_order = jnp.argsort(my_slots)
    ordered = jnp.take(columns, send_order, axis=0)
    owned_cols = lax.all_to_all(ordered, "dp", split_axis=0, concat_axis=1, tiled=True)
    square_sum = lax.psum(jnp.sum(jnp.square(gradients.astype(jnp.float32))), ("dp", "mp"))
    clip_scale = jnp.minimum(
        jnp.float32(1.0), rms_limit / jnp.sqrt(square_sum / (MATRICES * D * FF) + epsilon)
    )
    owned_count = owned_cols.shape[0]
    owned_blocks = owned_cols.reshape(owned_count, D // BLOCK, BLOCK, BLOCK)
    left_root = left_roots[:, 0]
    right_root = right_roots[:, 0]
    first_product = jnp.einsum(
        "snab,snbc->snac", left_root, owned_blocks, preferred_element_type=jnp.float32
    )
    scaled = (clip_scale * first_product).astype(jnp.bfloat16)
    second_product = jnp.einsum(
        "snab,snbc->snac", scaled, right_root, preferred_element_type=jnp.float32
    )
    finished = second_product.astype(jnp.bfloat16).reshape(owned_count, D, BLOCK)
    returned = lax.all_to_all(finished, "dp", split_axis=1, concat_axis=0, tiled=True)
    restored = jnp.take(returned, my_slots, axis=0)
    update = (
        restored.reshape(MATRICES, local_cols, row_count, BLOCK)
        .transpose(0, 2, 1, 3)
        .reshape(MATRICES, row_count, local_cols * BLOCK)
    )
    return (update, clip_scale)


def solution(mesh):
    return jax.shard_map(
        body,
        mesh=mesh,
        in_specs=(
            P(None, "dp", "mp"),
            P(),
            P("dp", "mp", None, None, None),
            P("dp", "mp", None, None, None),
        ),
        out_specs=(P(None, "dp", "mp"), P()),
        check_vma=False,
    )
```

profile of v0, /device:TPU:0, one launch (start us, length us, event | category | flops | bytes accessed | tf_op | source)
XLA Modules:
  0.0 1468.3 jit_solution(521979596373554846)
XLA Ops:
  0.6 0.0 copy-start
  0.7 0.7 copy-done
  1.3 0.1 constant_dynamic-slice_fusion
  1.4 0.1 reshape.30
  1.5 1.6 sort.17
  3.1 17.6 %fusion.8 = (bf16[8,448,896]{2,1,0:T(8,128)(2,1)}, bf16[8,448,896]{2,1,0:T(8,128)(2,1)}, bf16[8,448,896]{2,1,0:T(8,128)(2,1)}, bf16[8,448,896]{2,1,0:T(8,128)(2,1)}) fusion(bf16[8,448,3584]{2,1,0:T(8,128)(2,1)} %param.6), kind=kLoop, calls=%fused_computation.18 | loop fusion | bytes 51380224 | tf_op jit(solution)/shard_map/slice
  20.8 18.6 %pad_maximum_fusion = bf16[8,1792,896]{2,1,0:T(8,128)(2,1)} fusion(bf16[8,448,896]{2,1,0:T(8,128)(2,1)} %get-tuple-element.7, bf16[8,448,896]{2,1,0:T(8,128)(2,1)} %get-tuple-element.8, bf16[8,448,896]{2,1,0:T(8,128)(2,1)} %get-tuple-element.6, bf16[8,448,896]{2,1,0:T(8,128)(2,1)} %get-tuple-element.5), kind=kLoop, calls=%fused_computation.4 | loop fusion | flops 102760448 | bytes 51380224 | tf_op jit(solution)/shard_map/concatenate
  39.4 18.9 %gather_fusion = bf16[32,448,896]{2,1,0:T(8,128)(2,1)} fusion(bf16[32,448,896]{2,1,0:T(8,128)(2,1)} %bitcast.34, s32[1024]{0:T(1024)S(1)} %pad_clamp_fusion.1), kind=kCustom, calls=%fused_computation.clone | custom fusion | bytes 51380352 | tf_op jit(solution)/shard_map/jit(_take)/gather | solution.py:28
  58.3 21.6 %broadcast_select_fusion.1 = bf16[32,448,896]{2,1,0:T(8,128)(2,1)} fusion(bf16[32,448,896]{2,1,0:T(8,128)(2,1)} %gather_fusion, pred[32]{0:T(512)(128)(4,1)S(1)} %compare_and_fusion.1), kind=kLoop, calls=%fused_computation.9 | loop fusion | flops 12845056 | bytes 51380256 | tf_op jit(solution)/shard_map/jit(_take)/select_n | solution.py:28
  79.8 7.3 all-to-all-start
  87.1 15.9 %multiply_reduce_fusion = f32[]{:T(128)} fusion(bf16[8,448,3584]{2,1,0:T(8,128)(2,1)} %param.6), kind=kLoop, calls=%fused_computation.3 | loop fusion | flops 38535168 | bytes 25690116 | tf_op jit(solution)/shard_map/reduce_sum | solution.py:30
  103.0 559.1 %psum.7 = f32[]{:T(128)} all-reduce(f32[]{:T(128)} %multiply_reduce_fusion), channel_id=1, replica_groups=mesh['dp'=8,'mp'=4] {'dp','mp'}, use_global_device_ids=true, to_apply=%region_1.2 | all-reduce | flops 1 | bytes 8 | tf_op jit(solution)/shard_map/psum | solution.py:30
  662.8 21.0 %copy.11 = bf16[4,8,448,896]{3,2,1,0:T(8,128)(2,1)} copy(bf16[4,8,448,896]{3,2,0,1:T(8,128)(2,1)} %bitcast.2) | data formatting | bytes 51380224 | tf_op jit(solution)/shard_map/all_to_all | solution.py:29
  683.8 43.5 %multiply_convert_fusion.clone.4 = bf16[4,4,896,896]{3,2,1,0:T(8,128)(2,1)} fusion(bf16[4,4,896,896]{3,2,1,0:T(8,128)(2,1)} %bitcast.39, bf16[4,1,4,896,896]{4,3,2,1,0:T(8,128)(2,1)} %param.8, f32[]{:T(128)} %min_shard_map.3), kind=kOutput, calls=%fused_computation.2.clone.clone.clone.1 | convolution fusion | flops 23044030464 | bytes 77070336 | tf_op jit(solution)/shard_map/snab,snbc->snac/dot_general | solution.py:38
  727.3 43.5 %fusion.3 = bf16[4,4,896,896]{3,2,1,0:T(8,128)(2,1)} fusion(bf16[4,1,4,896,896]{4,3,2,1,0:T(8,128)(2,1)} %param.9, bf16[4,4,896,896]{3,2,1,0:T(8,128)(2,1)} %multiply_convert_fusion.clone.4), kind=kOutput, calls=%fused_computation.10 | convolution fusion | flops 23031185408 | bytes 77070336 | tf_op jit(solution)/shard_map/snab,snbc->snac/dot_general | solution.py:42
  770.8 56.9 %copy.14 = bf16[4,3584,896]{2,0,1:T(4,128)(2,1)} copy(bf16[4,3584,896]{2,1,0:T(8,128)(2,1)} %bitcast.40) | data formatting | bytes 51380224 | tf_op jit(solution)/shard_map/reshape | solution.py:45
  827.7 6.5 all-to-all-start.1
  834.2 553.4 %all-to-all-done.1 = bf16[4,3584,896]{2,0,1:T(4,128)(2,1)} async-done(((bf16[4,3584,896]{2,0,1:T(4,128)(2,1)}), bf16[4,3584,896]{2,0,1:T(4,128)(2,1)}, u32[]{:S(2)}, u32[]{:S(2)}) %all-to-all-start.1) | async-done | bytes 25690144 | tf_op jit(solution)/shard_map/all_to_all | solution.py:46
  1387.7 17.5 %copy.15 = bf16[4,3584,896]{2,1,0:T(8,128)(2,1)} copy(bf16[4,3584,896]{2,0,1:T(4,128)(2,1)} %all-to-all-done.1) | data formatting | bytes 51380224 | tf_op jit(solution)/shard_map/all_to_all | solution.py:46
  1405.2 21.0 %copy.16 = bf16[8,4,448,896]{3,2,1,0:T(8,128)(2,1)} copy(bf16[8,4,448,896]{3,2,0,1:T(8,128)(2,1)} %bitcast.37) | data formatting | bytes 51380224 | tf_op jit(solution)/shard_map/all_to_all | solution.py:46
  1426.2 19.2 %gather_fusion.1 = bf16[32,448,896]{2,1,0:T(8,128)(2,1)} fusion(bf16[32,448,896]{2,1,0:T(8,128)(2,1)} %bitcast.35, s32[1024]{0:T(1024)S(1)} %pad_clamp_fusion), kind=kCustom, calls=%fused_computation.1.clone | custom fusion | bytes 51380352 | tf_op jit(solution)/shard_map/jit(_take)/gather | solution.py:47
  1445.4 12.9 broadcast_select_fusion
  1458.3 0.0 copy-start.1
  1458.3 8.8 copy.20
  (13 shorter events, 0.0 us)
Async XLA Ops:
  0.6 0.7 copy-start
  1.5 1.6 copy-start.2
  79.8 583.0 %all-to-all-start = ((bf16[32,448,896]{2,1,0:T(8,128)(2,1)}), bf16[32,448,896]{2,1,0:T(8,128)(2,1)}, u32[]{:S(2)}, u32[]{:S(2)}) async-start(bf16[32,448,896]{2,1,0:T(8,128)(2,1)} %broadcast_select_fusion.1), calls=%async_computation | async-start | bytes 51380224 | tf_op jit(solution)/shard_map/all_to_all | solution.py:29
  827.7 6.5 copy-start.3
  827.7 560.0 %all-to-all-start.1 = ((bf16[4,3584,896]{2,0,1:T(4,128)(2,1)}), bf16[4,3584,896]{2,0,1:T(4,128)(2,1)}, u32[]{:S(2)}, u32[]{:S(2)}) async-start(bf16[4,3584,896]{2,0,1:T(4,128)(2,1)} %copy.14), calls=%async_computation.1 | async-start | bytes 51380224 | tf_op jit(solution)/shard_map/all_to_all | solution.py:46
  1458.3 8.8 copy-start.1
where the time goes:
time: 1470 us
  blocking collectives  559 us (38%)
  waiting for transfers between devices  553 us (38%)
  local copies, waits for them, and re-layouts  182 us (12%)
  matrix products  87 us (6%)
  other arithmetic  70.6 us (5%)
    psum x1, blocking collectives, body(): lax.psum(jnp.sum(jnp.square(gradients.astype(jnp.float32))), ('dp', 'mp'))  559 us
    all_to_all x1, waiting for transfers between devices, body(): lax.all_to_all(finished, 'dp', split_axis=1, concat_axis=0, tiled=True)  553 us
    reshape x1, local copies, waits for them, and re-layouts, body(): second_product.astype(jnp.bfloat16).reshape(owned_count, D, BLOCK)  56.9 us
    dot_general x1, matrix products, body(): jnp.einsum('snab,snbc->snac', scaled, right_root, preferred_element_type=...  43.5 us
    dot_general x1, matrix products, body(): jnp.einsum('snab,snbc->snac', left_root, owned_blocks, preferred_element_...  43.5 us
    all_to_all x2, local copies, waits for them, and re-layouts, body(): lax.all_to_all(finished, 'dp', split_axis=1, concat_axis=0, tiled=True)  38.5 us
  transfers between devices with their start and end apart: 2, of which 1 were waited for; matrix products, arithmetic and copies ran while one was open for 1% of the time, Pallas kernels for 0%

commit v1 on v0

--- a/solution.py
+++ b/solution.py
@@ -43,7 +43,10 @@
         "snab,snbc->snac", scaled, right_root, preferred_element_type=jnp.float32
     )
     finished = second_product.astype(jnp.bfloat16).reshape(owned_count, D, BLOCK)
-    returned = lax.all_to_all(finished, "dp", split_axis=1, concat_axis=0, tiled=True)
+    returned = jnp.concatenate(
+        lax.all_to_all(jnp.stack(jnp.split(finished, lax.axis_size("dp"), axis=1)), "dp", 0, 0),
+        axis=0,
+    )
     restored = jnp.take(returned, my_slots, axis=0)
     update = (
         restored.reshape(MATRICES, local_cols, row_count, BLOCK)

time: 1470 us -> 1400 us (0.952)
  local copies, waits for them, and re-layouts: 182 us -> 112 us
    reshape x1 -> x0, local copies, waits for them, and re-layouts: 56.9 us -> none  [body(): second_product.astype(jnp.bfloat16).reshape(owned_count, D, BLOCK)]
    all_to_all x2 -> x0, local copies, waits for them, and re-layouts: 38.5 us -> none  [body(): lax.all_to_all(finished, 'dp', split_axis=1, concat_axis=0, tiled=True)]
    unnamed x8 -> x17, local copies, waits for them, and re-layouts: 0.7 us -> 24.2 us
where the time goes in v1:
time: 1400 us
  blocking collectives  559 us (40%)
  waiting for transfers between devices  553 us (40%)
  local copies, waits for them, and re-layouts  112 us (8%)
  matrix products  87 us (6%)
  other arithmetic  70.6 us (5%)
    psum x1, blocking collectives, body(): lax.psum(jnp.sum(jnp.square(gradients.astype(jnp.float32))), ('dp', 'mp'))  559 us
    all_to_all x1, waiting for transfers between devices, body(): lax.all_to_all(jnp.stack(jnp.split(finished, lax.axis_size('dp'), axis=1)...  553 us
    dot_general x1, matrix products, body(): jnp.einsum('snab,snbc->snac', scaled, right_root, preferred_element_type=...  43.5 us
    dot_general x1, matrix products, body(): jnp.einsum('snab,snbc->snac', left_root, owned_blocks, preferred_element_...  43.5 us
  transfers between devices with their start and end apart: 2, of which 1 were waited for; matrix products, arithmetic and copies ran while one was open for 1% of the time, Pallas kernels for 0%

profile of v1, /device:TPU:0, one launch (start us, length us, event | category | flops | bytes accessed | tf_op | source)
XLA Modules:
  0.0 1398.4 jit_solution(988415917645018472)
XLA Ops:
  1.5 1.6 sort.17
  3.1 17.6 %fusion.16 = (bf16[8,448,896]{2,1,0:T(8,128)(2,1)}, bf16[8,448,896]{2,1,0:T(8,128)(2,1)}, bf16[8,448,896]{2,1,0:T(8,128)(2,1)}, bf16[8,448,896]{2,1,0:T(8,128)(2,1)}) fusion(bf16[8,448,3584]{2,1,0:T(8,128)(2,1)} %param.6), kind=kLoop, calls=%fused_computation.34 | loop fusion | bytes 51380224 | tf_op jit(solution)/shard_map/slice
  20.8 18.6 %pad_maximum_fusion = bf16[8,1792,896]{2,1,0:T(8,128)(2,1)} fusion(bf16[8,448,896]{2,1,0:T(8,128)(2,1)} %get-tuple-element.7, bf16[8,448,896]{2,1,0:T(8,128)(2,1)} %get-tuple-element.8, bf16[8,448,896]{2,1,0:T(8,128)(2,1)} %get-tuple-element.6, bf16[8,448,896]{2,1,0:T(8,128)(2,1)} %get-tuple-element.5), kind=kLoop, calls=%fused_computation.4 | loop fusion | flops 102760448 | bytes 51380224 | tf_op jit(solution)/shard_map/concatenate
  39.4 18.9 %gather_fusion = bf16[32,448,896]{2,1,0:T(8,128)(2,1)} fusion(bf16[32,448,896]{2,1,0:T(8,128)(2,1)} %bitcast.63, s32[1024]{0:T(1024)S(1)} %pad_clamp_fusion.1), kind=kCustom, calls=%fused_computation.clone | custom fusion | bytes 51380352 | tf_op jit(solution)/shard_map/jit(_take)/gather | solution.py:28
  58.3 21.6 %broadcast_select_fusion.1 = bf16[32,448,896]{2,1,0:T(8,128)(2,1)} fusion(bf16[32,448,896]{2,1,0:T(8,128)(2,1)} %gather_fusion, pred[32]{0:T(512)(128)(4,1)S(1)} %compare_and_fusion.1), kind=kLoop, calls=%fused_computation.9 | loop fusion | flops 12845056 | bytes 51380256 | tf_op jit(solution)/shard_map/jit(_take)/select_n | solution.py:28
  79.8 7.3 all-to-all-start
  87.1 15.9 %multiply_reduce_fusion = f32[]{:T(128)} fusion(bf16[8,448,3584]{2,1,0:T(8,128)(2,1)} %param.6), kind=kLoop, calls=%fused_computation.3 | loop fusion | flops 38535168 | bytes 25690116 | tf_op jit(solution)/shard_map/reduce_sum | solution.py:30
  103.0 559.1 %psum.7 = f32[]{:T(128)} all-reduce(f32[]{:T(128)} %multiply_reduce_fusion), channel_id=1, replica_groups=mesh['dp'=8,'mp'=4] {'dp','mp'}, use_global_device_ids=true, to_apply=%region_1.2 | all-reduce | flops 1 | bytes 8 | tf_op jit(solution)/shard_map/psum | solution.py:30
  662.8 21.0 %copy.6 = bf16[4,8,448,896]{3,2,1,0:T(8,128)(2,1)} copy(bf16[4,8,448,896]{3,2,0,1:T(8,128)(2,1)} %bitcast.2) | data formatting | bytes 51380224 | tf_op jit(solution)/shard_map/all_to_all | solution.py:29
  683.8 43.5 %multiply_convert_fusion.clone.4 = bf16[4,4,896,896]{3,2,1,0:T(8,128)(2,1)} fusion(bf16[4,4,896,896]{3,2,1,0:T(8,128)(2,1)} %bitcast.74, bf16[4,1,4,896,896]{4,3,2,1,0:T(8,128)(2,1)} %param.8, f32[]{:T(128)} %min_shard_map.3), kind=kOutput, calls=%fused_computation.2.clone.clone.clone.1 | convolution fusion | flops 23044030464 | bytes 77070336 | tf_op jit(solution)/shard_map/snab,snbc->snac/dot_general | solution.py:38
  727.3 43.5 %fusion.3 = bf16[4,4,896,896]{3,2,1,0:T(8,128)(2,1)} fusion(bf16[4,1,4,896,896]{4,3,2,1,0:T(8,128)(2,1)} %param.9, bf16[4,4,896,896]{3,2,1,0:T(8,128)(2,1)} %multiply_convert_fusion.clone.4), kind=kOutput, calls=%fused_computation.10 | convolution fusion | flops 23031185408 | bytes 77070336 | tf_op jit(solution)/shard_map/snab,snbc->snac/dot_general | solution.py:42
  770.9 4.0 fusion.13
  774.8 4.6 fusion.12
  779.5 4.6 fusion.11
  784.0 4.4 fusion.10
  788.4 1.9 fusion.9
  790.3 2.0 fusion.8
  792.3 2.0 fusion.7
  794.3 1.9 fusion.6
  796.2 6.6 all-to-all-start.1
  802.9 553.4 %all-to-all-done.1 = bf16[8,4,448,896]{3,2,1,0:T(8,128)(2,1)} async-done(((bf16[8,4,448,896]{3,2,1,0:T(8,128)(2,1)}), bf16[8,4,448,896]{3,2,1,0:T(8,128)(2,1)}, u32[]{:S(2)}, u32[]{:S(2)}) %all-to-all-start.1) | async-done | bytes 25690144 | tf_op jit(solution)/shard_map/all_to_all | solution.py:47
  1356.3 19.2 %gather_fusion.1 = bf16[32,448,896]{2,1,0:T(8,128)(2,1)} fusion(bf16[32,448,896]{2,1,0:T(8,128)(2,1)} %bitcast.15, s32[1024]{0:T(1024)S(1)} %pad_clamp_fusion), kind=kCustom, calls=%fused_computation.1.clone | custom fusion | bytes 51380352 | tf_op jit(solution)/shard_map/jit(_take)/gather | solution.py:50
  1375.5 12.9 broadcast_select_fusion
  1388.4 8.8 copy.12
  (20 shorter events, 0.9 us)
Async XLA Ops:
  0.6 0.7 copy-start
  1.5 1.6 copy-start.3
  79.8 583.0 %all-to-all-start = ((bf16[32,448,896]{2,1,0:T(8,128)(2,1)}), bf16[32,448,896]{2,1,0:T(8,128)(2,1)}, u32[]{:S(2)}, u32[]{:S(2)}) async-start(bf16[32,448,896]{2,1,0:T(8,128)(2,1)} %broadcast_select_fusion.1), calls=%async_computation | async-start | bytes 51380224 | tf_op jit(solution)/shard_map/all_to_all | solution.py:29
  770.8 17.6 %copy-start.2 = (bf16[4,4,896,896]{3,2,1,0:T(8,128)(2,1)S(1)}, bf16[4,4,896,896]{3,2,1,0:T(8,128)(2,1)}, u32[]{:S(2)}) copy-start(bf16[4,4,896,896]{3,2,1,0:T(8,128)(2,1)} %fusion.3) | copy-start | bytes 77070336
  796.2 6.6 copy-start.4
  796.2 560.1 %all-to-all-start.1 = ((bf16[8,4,448,896]{3,2,1,0:T(8,128)(2,1)}), bf16[8,4,448,896]{3,2,1,0:T(8,128)(2,1)}, u32[]{:S(2)}, u32[]{:S(2)}) async-start(bf16[8,4,448,896]{3,2,1,0:T(8,128)(2,1)} %fusion.6), calls=%async_computation.1 | async-start | bytes 51380224 | tf_op jit(solution)/shard_map/all_to_all | solution.py:47
  1388.4 8.8 copy-start.1
